TPU v7x, 32 devices: a whole 2x2x4 slice. The times are simulated.
32 devices in a mesh: rows: 8 (over y, x, core), cols: 4 (over z).
Axes of the slice: x: 2, y: 2, z: 4, core: 2. Of those that a mesh axis runs over, the one named last changes fastest.
Arguments:
- projection: float32 [4096, 65536], P('rows', 'cols'), may hold values from -0.09375 to 0.09375
- basis: float32 [128, 65536], P(None, ('cols', 'rows')), may hold values from -6 to 6
Outputs:
- new_block: float32 [16, 65536], P(None, ('cols', 'rows'))
- coefficients: float32 [128, 16], replicated
- factor: float32 [16, 16], replicated
All inputs are finite; a program needn't handle non-finite values.
Results may differ from a plain program's by a relative error of at most 0.0029.
Values sent between devices are 32-bit elements; how exact they have to be, the bound alone decides.
No kernel may reach another device: no remote copies, remote signals or barrier semaphores. Data moves between devices by JAX's collectives and lax.ppermute only.
A program may use at most 64 MiB of HBM per device.

v0:
```python
import jax
import jax.numpy as jnp
from jax import lax
from jax.sharding import PartitionSpec as P

N = 65536
BS = 16


def contract(left, right):
    return lax.dot_general(
        left,
        right,
        (((1,), (1,)), ((), ())),
        precision=lax.Precision.HIGHEST,
        preferred_element_type=jnp.float32,
    )


def matmul(left, right):
    return jnp.dot(left, right, precision=lax.Precision.HIGHEST, preferred_element_type=jnp.float32)


def wide_reduce(values):
    return lax.psum(values, ("rows", "cols"))


def orthogonalize(vectors, image, reducer):
    cross, correlation, self_gram = reducer(
        (contract(vectors, image), contract(vectors, vectors), contract(image, image))
    )
    cross = cross / N
    correlation = correlation / N
    self_gram = self_gram / N
    coeffs = cross + (cross - matmul(correlation, cross))
    gram_matrix = (
        self_gram
        - matmul(cross.T, coeffs)
        - matmul(coeffs.T, cross)
        + matmul(coeffs.T, matmul(correlation, coeffs))
    )
    image_two = image - matmul(coeffs.T, vectors)
    factor = jnp.linalg.cholesky(gram_matrix)
    new_block = jax.scipy.linalg.solve_triangular(factor, image_two, lower=True)
    return (new_block, coeffs, factor)


def local(projection, basis):
    current = basis[basis.shape[0] - BS :]
    partial_value = contract(lax.all_gather(current, "rows", axis=1, tiled=True), projection)
    projected = lax.psum(partial_value, "cols")
    image = matmul(projected, projection)
    adjoint = lax.psum_scatter(image, "rows", scatter_dimension=1, tiled=True)
    return orthogonalize(basis, adjoint, wide_reduce)


def solution(mesh):
    placed = (P("rows", "cols"), P(None, ("cols", "rows")))
    return jax.shard_map(
        local,
        mesh=mesh,
        in_specs=placed,
        out_specs=(P(None, ("cols", "rows")), P(), P()),
        check_vma=False,
    )
```

profile of v0, /device:TPU:1, one launch (start us, length us, event | category | flops | bytes accessed | tf_op | source)
XLA Modules:
  0.0 251.2 jit_solution(9730778745734969005)
XLA Ops:
  8.0 0.0 all-gather.2.cloned.1.call-start
  8.0 1.6 slice.15
  9.6 0.0 all-gather.2.cloned.1.call-update
  9.6 0.0 copy-start
  9.7 0.0 reduce-scatter.2.cloned.1.call-start
  9.7 27.4 %all-gather.2.cloned.1.call-done = f32[16,16384]{1,0:T(8,128)} async-done(((f32[16,2048]{1,0:T(8,128)}), f32[16,16384]{1,0:T(8,128)}) %all-gather.2.cloned.1.call-update) | async-done | bytes 1048592 | tf_op jit(solution)/shard_map/all_gather | solution.py:50
  37.1 33.1 %fusion.19 = f32[16,512]{1,0:T(8,128)S(1)} fusion(f32[16,16384]{1,0:T(8,128)} %all-gather.2.cloned.1.call-done, f32[512,16384]{1,0:T(8,128)} %param.2), kind=kOutput, calls=%fused_computation.32 | convolution fusion | flops 1610612736 | bytes 34635776 | tf_op jit(solution)/shard_map/dot_general | solution.py:11
  70.3 15.2 %psum.28 = f32[16,512]{1,0:T(8,128)S(1)} all-reduce(f32[16,512]{1,0:T(8,128)S(1)} %fusion.19), channel_id=1, replica_groups=mesh['rows'=8,'cols'=4] {'cols'}, use_global_device_ids=true, to_apply=%region_0.0 | all-reduce | flops 8192 | bytes 65536 | tf_op jit(solution)/shard_map/psum | solution.py:51
  85.5 20.3 %fusion.20 = f32[16,16384]{1,0:T(8,128)} fusion(f32[16,512]{1,0:T(8,128)S(1)} %psum.28, f32[512,16384]{1,0:T(8,128)} %param.2), kind=kOutput, calls=%fused_computation.33 | convolution fusion | flops 1610612736 | bytes 34635776 | tf_op jit(solution)/shard_map/dot_general | solution.py:21
  105.8 0.0 reduce-scatter.2.cloned.1.call-update
  105.9 0.0 all-reduce.3.cloned.1.call-start
  105.9 0.0 copy-done
  105.9 1.6 fusion.22
  107.5 0.0 all-reduce.3.cloned.1.call-update
  107.6 34.7 %reduce-scatter.2.cloned.1.call-done = f32[16,2048]{1,0:T(8,128)} async-done(((f32[16,16384]{1,0:T(8,128)}), f32[16,2048]{1,0:T(8,128)}) %reduce-scatter.2.cloned.1.call-update) | async-done | bytes 131088 | tf_op jit(solution)/shard_map/reduce_scatter | solution.py:53
  142.3 1.8 convolution_bitcast_fusion
  144.1 1.2 fusion.21
  145.3 39.0 %all-reduce = (f32[128,16]{0,1:T(8,128)S(1)}, f32[16,16]{0,1:T(8,128)S(1)}) all-reduce(f32[128,16]{0,1:T(8,128)S(1)} %convolution_bitcast_fusion, f32[16,16]{0,1:T(8,128)S(1)} %fusion.21), channel_id=1, replica_groups=mesh['rows'=8,'cols'=4] {'rows','cols'}, use_global_device_ids=true, to_apply=%region_3.0 | all-reduce | flops 2304 | bytes 18432 | tf_op jit(solution)/shard_map/psum | solution.py:25
  184.4 49.6 %all-reduce.3.cloned.1.call-done = f32[128,128]{1,0:T(8,128)} async-done(((f32[128,128]{1,0:T(8,128)}), f32[128,128]{1,0:T(8,128)}) %all-reduce.3.cloned.1.call-update) | async-done | bytes 65552 | tf_op jit(solution)/shard_map/psum | solution.py:25
  233.9 1.0 fusion
  235.0 0.0 copy-start.1
  235.0 0.1 convolution_subtract_fusion.3
  235.1 0.1 convolution_subtract_fusion.2
  235.3 1.0 fusion.1
  236.3 0.2 convolution_add_fusion
  236.5 0.1 copy.9
  236.6 1.5 cholesky.16
  238.1 0.6 compare_reduce_fusion
  238.8 1.2 select_bitcast_fusion
  240.0 1.2 custom-call.7
  241.3 1.5 convolution_subtract_fusion
  242.8 1.0 fusion.6
  243.8 0.0 copy-done.1
  (2 shorter events, 0.0 us)
Async XLA Ops:
  8.0 29.1 %all-gather.2.cloned.1.call-start = ((), (), s32[]{:S(2)}) async-start(), calls=%async_computation.1 | async-start | bytes 1179648 | tf_op jit(solution)/shard_map/all_gather | solution.py:50
  9.6 96.3 %copy-start = (f32[128,2048]{1,0:T(8,128)S(1)}, f32[128,2048]{1,0:T(8,128)}, u32[]{:S(2)}) copy-start(f32[128,2048]{1,0:T(8,128)} %param.3) | copy-start | bytes 3145732
  9.7 132.6 %reduce-scatter.2.cloned.1.call-start = ((), (), s32[]{:S(2)}) async-start(), calls=%async_computation.2 | async-start | bytes 1179648 | tf_op jit(solution)/shard_map/reduce_scatter | solution.py:53
  105.9 128.1 %all-reduce.3.cloned.1.call-start = ((), (), s32[]{:S(2)}) async-start(), calls=%async_computation.3 | async-start | bytes 131072 | tf_op jit(solution)/shard_map/psum | solution.py:25
  235.0 8.8 %copy-start.1 = (f32[128,16]{0,1:T(8,128)}, f32[128,16]{0,1:T(8,128)S(1)}, u32[]{:S(2)}) copy-start(f32[128,16]{0,1:T(8,128)S(1)} %fusion) | copy-start | bytes 24580
Sparse Core Ops, SparseCore 0:
  11.3 25.8 all-gather.1
  106.0 36.2 reduce-scatter.1
Sparse Core Ops, SparseCore 1:
  112.5 121.4 all-reduce.2
where the time goes:
time: 252 us; the launch traced here: 251 us
  waiting for transfers between devices  112 us (44%)
  matrix products  63.2 us (25%)
  blocking collectives  54.3 us (22%)
  between operations  15.6 us (6%)
  other arithmetic  4.65 us (2%)
    psum x1, waiting for transfers between devices, wide_reduce(): return lax.psum(values, ('rows', 'cols'))  49.6 us
    psum x1, blocking collectives, wide_reduce(): return lax.psum(values, ('rows', 'cols'))  39 us
    dot_general x4, matrix products, contract(): lax.dot_general(left, right, (((1,), (1,)), ((), ())), precision=lax.Prec...  37.8 us
    reduce_scatter x1, waiting for transfers between devices, local(): adjoint = lax.psum_scatter(image, 'rows', scatter_dimension=1, tiled=True)  34.7 us
    all_gather x1, waiting for transfers between devices, local(): lax.all_gather(current, 'rows', axis=1, tiled=True)  27.4 us
    dot_general x7, matrix products, matmul(): jnp.dot(left, right, precision=lax.Precision.HIGHEST, preferred_element_t...  24.4 us
    psum x1, blocking collectives, local(): projected = lax.psum(partial_value, 'cols')  15.2 us
  transfers between devices with their start and end apart: 3, of which 3 were waited for; matrix products, arithmetic and copies ran while one was open for 2% of the time, Pallas kernels for 0%

commit v1 on v0

--- a/solution.py
+++ b/solution.py
@@ -47,7 +47,12 @@
 
 def local(projection, basis):
     current = basis[basis.shape[0] - BS :]
-    partial_value = contract(lax.all_gather(current, "rows", axis=1, tiled=True), projection)
+    partial_value = contract(
+        jnp.concatenate(
+            lax.all_to_all(jnp.stack([current] * lax.axis_size("rows")), "rows", 0, 0), axis=1
+        ),
+        projection,
+    )
     projected = lax.psum(partial_value, "cols")
     image = matmul(projected, projection)
     adjoint = lax.psum_scatter(image, "rows", scatter_dimension=1, tiled=True)

time: 252 us -> 241 us (0.956)
  waiting for transfers between devices: 112 us -> 84.3 us
  blocking collectives: 54.3 us -> 73.6 us
    all_gather x1 -> x0, waiting for transfers between devices: 27.4 us -> none  [local(): lax.all_gather(current, 'rows', axis=1, tiled=True)]
    all_to_all x0 -> x1, blocking collectives: none -> 19.1 us  [local(): lax.all_to_all(jnp.stack([current] * lax.axis_size('rows')), 'rows', 0, 0)]
  transfers between devices with their start and end apart: 3 -> 2, of which waited for: 3 -> 2; matrix products, arithmetic and copies ran while one was open for 2% -> 2% of each run, Pallas kernels for 0% -> 0%
where the time goes in v1:
time: 241 us
  waiting for transfers between devices  84.3 us (35%)
  blocking collectives  73.6 us (31%)
  matrix products  60.9 us (25%)
  between operations  15.6 us (6%)
  other arithmetic  4.62 us (2%)
    psum x1, waiting for transfers between devices, wide_reduce(): return lax.psum(values, ('rows', 'cols'))  49.6 us
    psum x1, blocking collectives, wide_reduce(): return lax.psum(values, ('rows', 'cols'))  39 us
    dot_general x4, matrix products, contract(): lax.dot_general(left, right, (((1,), (1,)), ((), ())), precision=lax.Prec...  35.6 us
    reduce_scatter x1, waiting for transfers between devices, local(): adjoint = lax.psum_scatter(image, 'rows', scatter_dimension=1, tiled=True)  34.7 us
    dot_general x7, matrix products, matmul(): jnp.dot(left, right, precision=lax.Precision.HIGHEST, preferred_element_t...  24.3 us
    all_to_all x1, blocking collectives, local(): lax.all_to_all(jnp.stack([current] * lax.axis_size('rows')), 'rows', 0, 0)  19.1 us
    psum x1, blocking collectives, local(): projected = lax.psum(partial_value, 'cols')  15.5 us
  transfers between devices with their start and end apart: 2, of which 2 were waited for; matrix products, arithmetic and copies ran while one was open for 2% of the time, Pallas kernels for 0%

profile of v1, /device:TPU:1, one launch (start us, length us, event | category | flops | bytes accessed | tf_op | source)
XLA Modules:
  0.0 240.5 jit_solution(16231036406213487614)
XLA Ops:
  8.0 0.0 reduce-scatter.2.cloned.1.call-start
  8.0 0.9 slice.15
  9.0 0.1 stack.2
  9.1 19.1 %all_to_all.5 = f32[8,16,2048]{2,1,0:T(8,128)S(1)} all-to-all(f32[8,16,2048]{2,1,0:T(8,128)S(1)} %stack.2), channel_id=1, replica_groups=mesh['rows'=8,'cols'=4] {'rows'}, dimensions={0} | all-to-all | bytes 2097152 | tf_op jit(solution)/shard_map/all_to_all | solution.py:52
  28.2 0.1 copy.25
  28.3 0.0 copy-start
  28.3 31.0 %fusion.19 = f32[16,512]{1,0:T(8,128)S(1)} fusion(f32[16,16384]{1,0:T(8,128)S(1)} %bitcast.32, f32[512,16384]{1,0:T(8,128)} %param.2), kind=kOutput, calls=%fused_computation.32 | convolution fusion | flops 1610612736 | bytes 34635776 | tf_op jit(solution)/shard_map/dot_general | solution.py:11
  59.3 15.5 %psum.28 = f32[16,512]{1,0:T(8,128)S(1)} all-reduce(f32[16,512]{1,0:T(8,128)S(1)} %fusion.19), channel_id=1, replica_groups=mesh['rows'=8,'cols'=4] {'cols'}, use_global_device_ids=true, to_apply=%region_0.0 | all-reduce | flops 8192 | bytes 65536 | tf_op jit(solution)/shard_map/psum | solution.py:56
  74.8 20.3 %fusion.20 = f32[16,16384]{1,0:T(8,128)} fusion(f32[16,512]{1,0:T(8,128)S(1)} %psum.28, f32[512,16384]{1,0:T(8,128)} %param.2), kind=kOutput, calls=%fused_computation.33 | convolution fusion | flops 1610612736 | bytes 34635776 | tf_op jit(solution)/shard_map/dot_general | solution.py:21
  95.1 0.0 reduce-scatter.2.cloned.1.call-update
  95.1 0.2 all-reduce.3.cloned.1.call-start
  95.3 0.0 copy-done
  95.3 1.6 fusion.22
  97.0 0.0 all-reduce.3.cloned.1.call-update
  97.0 34.7 %reduce-scatter.2.cloned.1.call-done = f32[16,2048]{1,0:T(8,128)} async-done(((f32[16,16384]{1,0:T(8,128)}), f32[16,2048]{1,0:T(8,128)}) %reduce-scatter.2.cloned.1.call-update) | async-done | bytes 131088 | tf_op jit(solution)/shard_map/reduce_scatter | solution.py:58
  131.7 1.8 convolution_bitcast_fusion
  133.5 1.2 fusion.21
  134.7 39.0 %all-reduce = (f32[128,16]{0,1:T(8,128)S(1)}, f32[16,16]{0,1:T(8,128)S(1)}) all-reduce(f32[128,16]{0,1:T(8,128)S(1)} %convolution_bitcast_fusion, f32[16,16]{0,1:T(8,128)S(1)} %fusion.21), channel_id=1, replica_groups=mesh['rows'=8,'cols'=4] {'rows','cols'}, use_global_device_ids=true, to_apply=%region_3.0 | all-reduce | flops 2304 | bytes 18432 | tf_op jit(solution)/shard_map/psum | solution.py:25
  173.8 49.6 %all-reduce.3.cloned.1.call-done = f32[128,128]{1,0:T(8,128)} async-done(((f32[128,128]{1,0:T(8,128)}), f32[128,128]{1,0:T(8,128)}) %all-reduce.3.cloned.1.call-update) | async-done | bytes 65552 | tf_op jit(solution)/shard_map/psum | solution.py:25
  223.3 1.0 fusion
  224.4 0.0 copy-start.1
  224.4 0.1 convolution_subtract_fusion.3
  224.5 0.1 convolution_subtract_fusion.2
  224.7 1.0 fusion.1
  225.7 0.2 convolution_add_fusion
  225.9 0.1 copy.20
  226.0 1.5 cholesky.16
  227.5 0.6 compare_reduce_fusion
  228.1 1.2 select_bitcast_fusion
  229.4 1.2 custom-call.7
  230.6 1.5 convolution_subtract_fusion
  232.1 1.0 fusion.6
  233.1 0.0 copy-done.1
  (2 shorter events, 0.0 us)
Async XLA Ops:
  8.0 123.7 %reduce-scatter.2.cloned.1.call-start = ((), (), s32[]{:S(2)}) async-start(), calls=%async_computation.2 | async-start | bytes 1179648 | tf_op jit(solution)/shard_map/reduce_scatter | solution.py:58
  28.3 67.1 %copy-start = (f32[128,2048]{1,0:T(8,128)S(1)}, f32[128,2048]{1,0:T(8,128)}, u32[]{:S(2)}) copy-start(f32[128,2048]{1,0:T(8,128)} %param.3) | copy-start | bytes 3145732
  95.1 128.2 %all-reduce.3.cloned.1.call-start = ((), (), s32[]{:S(2)}) async-start(), calls=%async_computation.3 | async-start | bytes 131072 | tf_op jit(solution)/shard_map/psum | solution.py:25
  224.4 8.7 %copy-start.1 = (f32[128,16]{0,1:T(8,128)}, f32[128,16]{0,1:T(8,128)S(1)}, u32[]{:S(2)}) copy-start(f32[128,16]{0,1:T(8,128)S(1)} %fusion) | copy-start | bytes 24580
Sparse Core Ops, SparseCore 0:
  95.2 36.4 reduce-scatter.1
Sparse Core Ops, SparseCore 1:
  101.8 121.5 all-reduce.2
